TPU v7x, 32 devices: a whole 2x2x4 slice. The times are simulated.
32 devices in a mesh: row: 4 (over y, core), col: 8 (over z, x).
Axes of the slice: x: 2, y: 2, z: 4, core: 2. Of those that a mesh axis runs over, the one named last changes fastest.
Arguments:
- adjacency: int32 [8192, 8192], P('row', 'col'), may hold values from 0 to 1, as said below
Outputs:
- closure: bfloat16 [8192, 8192], P('row', 'col')
Inputs may be any that keep to these rules, and one draw needn't show every extreme that they name: `adjacency`: every entry is 0 or 1; there is no bound on the number of ones in a row, a column or a block, and their share differs widely between rows and between columns.
All inputs are finite; a program needn't handle non-finite values.
Results may differ from a plain program's by a relative error of at most 0.001.
Values may be sent and summed in bfloat16 or wider, within the bound.
A program may use at most 192 MiB of HBM per device.

v0:
```python
import jax
import jax.numpy as jnp
from jax import lax
from jax.sharding import PartitionSpec as P

PANEL = 512
PANELS = 4


def from_root(shard, axis, root):
    mine = lax.axis_index(axis) == root
    return lax.psum(jnp.where(mine, shard, jnp.zeros_like(shard)), axis)


def per_device(adjacency):
    block_rows, block_cols = adjacency.shape
    window = PANELS * PANEL
    left_parts = []
    for holder in range(-(-window // block_cols)):
        shared = adjacency.astype(jnp.bfloat16)
        left_parts.append(from_root(shared, "col", holder))
    holder = 0
    shared = adjacency.astype(jnp.bfloat16)
    right_parts = from_root(shared, "row", holder)
    left_whole = jnp.concatenate(left_parts, axis=1)
    totals = jnp.dot(left_whole, right_parts, preferred_element_type=jnp.float32)
    closure = jnp.where(totals > 0.5, 1.0, adjacency.astype(jnp.float32))
    return closure.astype(jnp.bfloat16)


def solution(mesh):
    in_specs = (P("row", "col"),)
    out_specs = P("row", "col")
    return jax.shard_map(
        per_device, mesh=mesh, in_specs=in_specs, out_specs=out_specs, check_vma=False
    )
```

profile of v0, /device:TPU:24, one launch (start us, length us, event | category | flops | bytes accessed | tf_op | source)
XLA Modules:
  0.0 393.7 jit_solution(16833688906265491029)
XLA Ops:
  6.5 0.0 all-reduce.4.cloned.1.call-start
  6.5 7.0 %broadcast_select_fusion.2 = (bf16[2048,1024]{1,0:T(8,128)(2,1)}, bf16[2048,1024]{1,0:T(8,128)(2,1)}, bf16[2048,1024]{1,0:T(8,128)(2,1)}) fusion(pred[]{:T(512)S(6)} %eq.9, s32[2048,1024]{1,0:T(8,128)} %param.1, pred[]{:T(512)S(6)} %eq.10, pred[]{:T(512)S(6)} %eq.11), kind=kLoop, calls=%fused_computation.7 | loop fusion | flops 8388608 | bytes 20971524 | tf_op jit(solution)/shard_map/jit(_where)/select_n | solution.py:12
  13.6 0.0 all-reduce.4.cloned.1.call-update
  13.6 0.0 all-reduce.6.cloned.1.call-start
  13.7 0.7 all-reduce.6.cloned.1.call-update
  14.4 85.9 %all-reduce.4.cloned.1.call-done = bf16[2048,1024]{1,0:T(8,128)(2,1)} async-done(((bf16[2048,1024]{1,0:T(8,128)(2,1)}), bf16[2048,1024]{1,0:T(8,128)(2,1)}) %all-reduce.4.cloned.1.call-update) | async-done | bytes 4194320 | tf_op jit(solution)/shard_map/psum | solution.py:12
  100.2 271.7 %all-reduce.6.cloned.1.call-done = (bf16[2048,1024]{1,0:T(8,128)(2,1)}, bf16[2048,1024]{1,0:T(8,128)(2,1)}) async-done(((bf16[2048,1024]{1,0:T(8,128)(2,1)}, bf16[2048,1024]{1,0:T(8,128)(2,1)}), (bf16[2048,1024]{1,0:T(8,128)(2,1)}, bf16[2048,1024]{1,0:T(8,128)(2,1)})) %all-reduce.6.cloned.1.call-update) | async-done | bytes 8388624 | tf_op jit(solution)/shard_map/psum | solution.py:12
  371.9 15.0 %select_convert_fusion = bf16[2048,1024]{1,0:T(8,128)(2,1)} fusion(s32[2048,1024]{1,0:T(8,128)} %param.1, bf16[2048,1024]{1,0:T(8,128)(2,1)} %all-reduce.4.cloned.1.call-done, bf16[2048,1024]{1,0:T(8,128)(2,1)} %get-tuple-element.5, bf16[2048,1024]{1,0:T(8,128)(2,1)} %get-tuple-element.6), kind=kOutput, calls=%fused_computation.4 | convolution fusion | flops 8615100416 | bytes 25165824 | tf_op jit(solution)/shard_map/dot_general | solution.py:26
Async XLA Ops:
  6.5 93.7 %all-reduce.4.cloned.1.call-start = ((), (), s32[]{:S(2)}) async-start(), calls=%async_computation | async-start | bytes 8388608 | tf_op jit(solution)/shard_map/psum | solution.py:12
  13.6 358.3 %all-reduce.6.cloned.1.call-start = ((), (), s32[]{:S(2)}) async-start(), calls=%async_computation.1 | async-start | bytes 16777216 | tf_op jit(solution)/shard_map/psum | solution.py:12
Sparse Core Ops, SparseCore 0:
  13.7 86.4 all-reduce.3
  104.3 267.5 all-reduce.5
where the time goes:
time: 398 us; the launch traced here: 394 us
  waiting for transfers between devices  358 us (90%)
  matrix products  15 us (4%)
  between operations  13.4 us (3%)
  other arithmetic  7.04 us (2%)
    psum x2, waiting for transfers between devices, from_root(): return lax.psum(jnp.where(mine, shard, jnp.zeros_like(shard)), axis)  358 us
    dot_general x1, matrix products, per_device(): jnp.dot(left_whole, right_parts, preferred_element_type=jnp.float32)  15 us
  transfers between devices with their start and end apart: 2, of which 2 were waited for; matrix products, arithmetic and copies ran while one was open for 0% of the time, Pallas kernels for 0%

commit v1 on v0

v1 whole, which is shorter than its diff:
```python
import functools

import jax
import jax.numpy as jnp
from jax import lax
from jax.experimental import pallas as pl
from jax.experimental.pallas import tpu as pltpu
from jax.sharding import PartitionSpec as P

PANEL = 512
PANELS = 4

CHUNK = 32
RIGHT = 64
GROUP = 256
TILE = 256
PER_STEP = 2
MESH = pl.DeviceIdType.MESH


def lag_of(row):
    return (5 * row) // 2


def kernel(n_rows, n_cols, window, adj_hbm, out, adj, left, right,
           adj_sem, z_send, z_recv, x_send, x_recv, r_send, r_recv):
    block_rows, block_cols = adj.shape
    holders = left.shape[0]
    stages = n_cols // holders
    n_chunks = block_rows // CHUNK
    n_adj = block_rows // RIGHT
    n_right = window // RIGHT
    n_groups = block_rows // GROUP
    n_tiles = block_cols // TILE
    units = n_groups * n_tiles
    per_group = GROUP // CHUNK

    r = lax.axis_index("row")
    c = lax.axis_index("col")
    hi = c // holders
    lo = lax.rem(c, holders)
    lag = lag_of(r)

    def adj_copy(i):
        rows = pl.ds(pl.multiple_of(i * RIGHT, RIGHT), RIGHT)
        return pltpu.make_async_copy(adj_hbm.at[rows], adj.at[rows], adj_sem.at[i])

    def chunk(j):
        return pl.ds(pl.multiple_of(j * CHUNK, CHUNK), CHUNK)

    def z_copy(j):
        part = left.at[lo, chunk(j)]
        return pltpu.make_async_remote_copy(
            src_ref=part, dst_ref=part, send_sem=z_send.at[j], recv_sem=z_recv.at[j],
            device_id={"col": c + holders}, device_id_type=MESH)

    def x_copy(d, j):
        part = left.at[lo, chunk(j)]
        peer = hi * holders + lax.rem(lo + d, holders)
        return pltpu.make_async_remote_copy(
            src_ref=part, dst_ref=part, send_sem=x_send.at[d - 1, j], recv_sem=x_recv.at[d - 1, j],
            device_id={"col": peer}, device_id_type=MESH)

    def x_arrival(d, j):
        part = left.at[lax.rem(lo + holders - d, holders), chunk(j)]
        peer = hi * holders + lax.rem(lo + holders - d, holders)
        return pltpu.make_async_remote_copy(
            src_ref=part, dst_ref=part, send_sem=x_send.at[d - 1, j], recv_sem=x_recv.at[d - 1, j],
            device_id={"col": peer}, device_id_type=MESH)

    def r_rows(i):
        return pl.ds(pl.multiple_of(i * RIGHT, RIGHT), RIGHT)

    def r_copy(i):
        part = right.at[r_rows(i)]
        return pltpu.make_async_remote_copy(
            src_ref=part, dst_ref=part, send_sem=r_send.at[i], recv_sem=r_recv.at[i],
            device_id={"row": r + 1}, device_id_type=MESH)

    @pl.loop(0, n_adj)
    def _(i):
        adj_copy(i).start()

    barrier = pltpu.get_barrier_semaphore()

    def greet(where):
        pl.semaphore_signal(barrier, inc=1, device_id=where, device_id_type=MESH)

    @pl.when(hi > 0)
    def _():
        greet({"col": c - holders})

    @pl.when(hi < stages - 1)
    def _():
        greet({"col": c + holders})

    for d in range(1, holders):
        greet({"col": hi * holders + lax.rem(lo + d, holders)})

    @pl.when(r > 0)
    def _():
        greet({"row": r - 1})

    @pl.when(r < n_rows - 1)
    def _():
        greet({"row": r + 1})

    def convert_left(j):
        left[lo, chunk(j), :] = adj[chunk(j), :].astype(jnp.bfloat16)

    def convert_right(i):
        right[r_rows(i), :] = adj[r_rows(i), :].astype(jnp.bfloat16)

    adj_copy(0).wait()

    @pl.when(hi == 0)
    def _():
        convert_left(0)

    @pl.when(r == 0)
    def _():
        convert_right(0)

    known = ((hi > 0).astype(jnp.int32) + (hi < stages - 1).astype(jnp.int32) + (holders - 1)
             + (r > 0).astype(jnp.int32) + (r < n_rows - 1).astype(jnp.int32))
    pl.semaphore_wait(barrier, known)

    def step(j):
        @pl.when(j + 1 < n_adj)
        def _():
            adj_copy(j + 1).wait()

        @pl.when((hi == 0) & (j + 1 < n_chunks))
        def _():
            convert_left(j + 1)

        @pl.when((r == 0) & (j + 1 < n_right))
        def _():
            convert_right(j + 1)

        @pl.when(hi > 0)
        def _():
            z_copy(j).wait_recv()

        @pl.when(hi < stages - 1)
        def _():
            z_copy(j).start()

        for d in range(1, holders):
            x_copy(d, j).start()

        i = j - lag

        @pl.when((i >= 0) & (i < n_right))
        def _():
            @pl.when(r > 0)
            def _():
                r_copy(i).wait_recv()

            @pl.when(r < n_rows - 1)
            def _():
                r_copy(i).start()

    def compute(u):
        g = u // n_tiles
        t = lax.rem(u, n_tiles)

        @pl.when(t == 0)
        def _():
            for d in range(1, holders):
                @pl.loop(0, per_group)
                def _(k):
                    x_arrival(d, g * per_group + k).wait_recv()

        rows = pl.ds(pl.multiple_of(g * GROUP, GROUP), GROUP)
        cols = pl.ds(pl.multiple_of(t * TILE, TILE), TILE)
        counts = jnp.zeros((GROUP, TILE), jnp.float32)
        for h in range(holders):
            counts += jnp.dot(left[h, rows, :], right[h * block_cols:(h + 1) * block_cols, cols],
                              preferred_element_type=jnp.float32)
        out[rows, cols] = jnp.where(counts > 0.5, 1, adj[rows, cols]).astype(out.dtype)

    body_units = units - n_tiles
    ready = n_right - 1 + lag_of(n_rows - 1)
    first = min(n_chunks, max(ready, n_chunks - 2 - -(-body_units // PER_STEP)))
    done = min(body_units, PER_STEP * (n_chunks - first))
    done -= done % PER_STEP

    @pl.loop(0, first)
    def _(j):
        step(j)

    @pl.loop(first, n_chunks)
    def _(j):
        step(j)
        for p in range(PER_STEP):
            u = (j - first) * PER_STEP + p

            @pl.when(u < done)
            def _():
                compute(u)

    @pl.loop(n_chunks, max(n_chunks, ready + 1))
    def _(j):
        i = j - lag

        @pl.when((i >= 0) & (i < n_right))
        def _():
            @pl.when(r > 0)
            def _():
                r_copy(i).wait_recv()

            @pl.when(r < n_rows - 1)
            def _():
                r_copy(i).start()

    @pl.loop(done, units)
    def _(u):
        compute(u)

    @pl.loop(0, n_chunks)
    def _(j):
        @pl.when(hi < stages - 1)
        def _():
            z_copy(j).wait_send()

        for d in range(1, holders):
            x_copy(d, j).wait_send()

    @pl.when(r < n_rows - 1)
    def _():
        @pl.loop(0, n_right)
        def _(i):
            r_copy(i).wait_send()


def per_device(n_rows, n_cols, adjacency):
    block_rows, block_cols = adjacency.shape
    window = PANELS * PANEL
    holders = window // block_cols
    n_chunks = block_rows // CHUNK
    dma = pltpu.SemaphoreType.DMA
    closed = pl.pallas_call(
        functools.partial(kernel, n_rows, n_cols, window),
        out_shape=jax.ShapeDtypeStruct((block_rows, block_cols), jnp.int8),
        in_specs=[pl.BlockSpec(memory_space=pl.ANY)],
        out_specs=pl.BlockSpec(memory_space=pltpu.VMEM),
        scratch_shapes=[
            pltpu.VMEM((block_rows, block_cols), jnp.int32),
            pltpu.VMEM((holders, block_rows, block_cols), jnp.bfloat16),
            pltpu.VMEM((window, block_cols), jnp.bfloat16),
            dma((block_rows // RIGHT,)),
            dma((n_chunks,)),
            dma((n_chunks,)),
            dma((holders - 1, n_chunks)),
            dma((holders - 1, n_chunks)),
            dma((window // RIGHT,)),
            dma((window // RIGHT,)),
        ],
        compiler_params=pltpu.CompilerParams(
            collective_id=0, has_side_effects=True, vmem_limit_bytes=58 * 1024 * 1024),
    )(adjacency)
    return closed.astype(jnp.bfloat16)


def solution(mesh):
    spec = P("row", "col")
    return jax.shard_map(
        functools.partial(per_device, mesh.shape["row"], mesh.shape["col"]),
        mesh=mesh, in_specs=(spec,), out_specs=spec, check_vma=False)
```

time: 398 us -> 114 us (0.29); the launches traced: 394 us -> 114 us
  waiting for transfers between devices: 358 us -> 0 us
  Pallas kernels: 0 us -> 110 us
  matrix products: 15 us -> 0 us
  between operations: 13.4 us -> 0.01 us
    psum x2 -> x0, waiting for transfers between devices: 358 us -> none  [from_root(): return lax.psum(jnp.where(mine, shard, jnp.zeros_like(shard)), axis)]
    pallas_call x0 -> x1, Pallas kernels: none -> 110 us  [per_device(): pl.pallas_call(functools.partial(kernel, n_rows, n_cols, window), out_sha...]
    dot_general x1 -> x0, matrix products: 15 us -> none  [per_device(): jnp.dot(left_whole, right_parts, preferred_element_type=jnp.float32)]
    select_n x1 -> x0, other arithmetic: 7.04 us -> none  [from_root(): return lax.psum(jnp.where(mine, shard, jnp.zeros_like(shard)), axis)]
    convert_element_type x0 -> x1, other arithmetic: none -> 4.65 us  [per_device(): return closed.astype(jnp.bfloat16)]
  transfers between devices with their start and end apart: 2 -> 0, of which waited for: 2 -> 0; matrix products, arithmetic and copies ran while one was open for 0% -> 0% of each run, Pallas kernels for 0% -> 0%
where the time goes in v1:
time: 114 us
  Pallas kernels  110 us (96%)
  other arithmetic  4.65 us (4%)
    pallas_call x1, Pallas kernels, per_device(): pl.pallas_call(functools.partial(kernel, n_rows, n_cols, window), out_sha...  110 us
    convert_element_type x1, other arithmetic, per_device(): return closed.astype(jnp.bfloat16)  4.65 us

profile of v1, /device:TPU:24, one launch (start us, length us, event | category | flops | bytes accessed | tf_op | source)
XLA Modules:
  0.0 114.2 jit_solution(6943255270689568190)
XLA Ops:
  0.0 109.5 %shard_map.17 = s8[2048,1024]{1,0:T(8,128)(4,1)} custom-call(s32[2048,1024]{1,0:T(8,128)} %adj_hbm.1), custom_call_target="tpu_custom_call" | custom-call | tf_op jit(solution)/shard_map/pallas_call | solution.py:243
  109.5 4.7 %convert_element_type.3 = bf16[2048,1024]{1,0:T(8,128)(2,1)} convert(s8[2048,1024]{1,0:T(8,128)(4,1)} %shard_map.17) | non-fusion elementwise | flops 2097152 | bytes 6291456 | tf_op jit(solution)/shard_map/convert_element_type | solution.py:263

commit v2 on v1

--- a/solution.py
+++ b/solution.py
@@ -51,21 +51,21 @@
     def z_copy(j):
         part = left.at[lo, chunk(j)]
         return pltpu.make_async_remote_copy(
-            src_ref=part, dst_ref=part, send_sem=z_send.at[j], recv_sem=z_recv.at[j],
+            src_ref=part, dst_ref=part, send_sem=z_send, recv_sem=z_recv.at[j],
             device_id={"col": c + holders}, device_id_type=MESH)
 
     def x_copy(d, j):
         part = left.at[lo, chunk(j)]
         peer = hi * holders + lax.rem(lo + d, holders)
         return pltpu.make_async_remote_copy(
-            src_ref=part, dst_ref=part, send_sem=x_send.at[d - 1, j], recv_sem=x_recv.at[d - 1, j],
+            src_ref=part, dst_ref=part, send_sem=x_send.at[d - 1], recv_sem=x_recv.at[d - 1, j],
             device_id={"col": peer}, device_id_type=MESH)
 
     def x_arrival(d, j):
         part = left.at[lax.rem(lo + holders - d, holders), chunk(j)]
         peer = hi * holders + lax.rem(lo + holders - d, holders)
         return pltpu.make_async_remote_copy(
-            src_ref=part, dst_ref=part, send_sem=x_send.at[d - 1, j], recv_sem=x_recv.at[d - 1, j],
+            src_ref=part, dst_ref=part, send_sem=x_send.at[d - 1], recv_sem=x_recv.at[d - 1, j],
             device_id={"col": peer}, device_id_type=MESH)
 
     def r_rows(i):
@@ -74,7 +74,7 @@
     def r_copy(i):
         part = right.at[r_rows(i)]
         return pltpu.make_async_remote_copy(
-            src_ref=part, dst_ref=part, send_sem=r_send.at[i], recv_sem=r_recv.at[i],
+            src_ref=part, dst_ref=part, send_sem=r_send, recv_sem=r_recv.at[i],
             device_id={"row": r + 1}, device_id_type=MESH)
 
     @pl.loop(0, n_adj)
@@ -218,20 +218,24 @@
     def _(u):
         compute(u)
 
-    @pl.loop(0, n_chunks)
-    def _(j):
-        @pl.when(hi < stages - 1)
-        def _():
-            z_copy(j).wait_send()
-
-        for d in range(1, holders):
-            x_copy(d, j).wait_send()
+    whole = left.at[lo]
+
+    @pl.when(hi < stages - 1)
+    def _():
+        pltpu.make_async_remote_copy(
+            src_ref=whole, dst_ref=whole, send_sem=z_send, recv_sem=z_recv.at[0],
+            device_id={"col": c + holders}, device_id_type=MESH).wait_send()
+
+    for d in range(1, holders):
+        pltpu.make_async_remote_copy(
+            src_ref=whole, dst_ref=whole, send_sem=x_send.at[d - 1], recv_sem=x_recv.at[d - 1, 0],
+            device_id={"col": hi * holders + lax.rem(lo + d, holders)}, device_id_type=MESH).wait_send()
 
     @pl.when(r < n_rows - 1)
     def _():
-        @pl.loop(0, n_right)
-        def _(i):
-            r_copy(i).wait_send()
+        pltpu.make_async_remote_copy(
+            src_ref=right, dst_ref=right, send_sem=r_send, recv_sem=r_recv.at[0],
+            device_id={"row": r + 1}, device_id_type=MESH).wait_send()
 
 
 def per_device(n_rows, n_cols, adjacency):
@@ -242,25 +246,25 @@
     dma = pltpu.SemaphoreType.DMA
     closed = pl.pallas_call(
         functools.partial(kernel, n_rows, n_cols, window),
-        out_shape=jax.ShapeDtypeStruct((block_rows, block_cols), jnp.int8),
-        in_specs=[pl.BlockSpec(memory_space=pl.ANY)],
+        out_shape=pltpu.VMEM((block_rows, block_cols), jnp.bfloat16),
+        in_specs=[pl.BlockSpec(memory_space=pltpu.HBM)],
         out_specs=pl.BlockSpec(memory_space=pltpu.VMEM),
         scratch_shapes=[
             pltpu.VMEM((block_rows, block_cols), jnp.int32),
             pltpu.VMEM((holders, block_rows, block_cols), jnp.bfloat16),
             pltpu.VMEM((window, block_cols), jnp.bfloat16),
             dma((block_rows // RIGHT,)),
+            dma,
             dma((n_chunks,)),
-            dma((n_chunks,)),
+            dma((holders - 1,)),
             dma((holders - 1, n_chunks)),
-            dma((holders - 1, n_chunks)),
-            dma((window // RIGHT,)),
+            dma,
             dma((window // RIGHT,)),
         ],
         compiler_params=pltpu.CompilerParams(
-            collective_id=0, has_side_effects=True, vmem_limit_bytes=58 * 1024 * 1024),
-    )(adjacency)
-    return closed.astype(jnp.bfloat16)
+            collective_id=0, has_side_effects=True, vmem_limit_bytes=40 * 1024 * 1024),
+    )(pltpu.with_memory_space_constraint(adjacency, pltpu.HBM))
+    return closed
 
 
 def solution(mesh):

time: 114 us -> 108 us (0.947)
  other arithmetic: 4.65 us -> 0 us
  Pallas kernels: 110 us -> 106 us
  local copies, waits for them, and re-layouts: 0 us -> 2.02 us
    convert_element_type x1 -> x0, other arithmetic: 4.65 us -> none  [per_device(): return closed.astype(jnp.bfloat16)]
    pallas_call x1, Pallas kernels: 110 us -> 106 us  [per_device(): pl.pallas_call(functools.partial(kernel, n_rows, n_cols, window), out_sha...]
    unnamed x0 -> x1, local copies, waits for them, and re-layouts: none -> 2.02 us
where the time goes in v2:
time: 108 us
  Pallas kernels  106 us (98%)
  local copies, waits for them, and re-layouts  2.02 us (2%)
    pallas_call x1, Pallas kernels, per_device(): pl.pallas_call(functools.partial(kernel, n_rows, n_cols, window), out_sha...  106 us

profile of v2, /device:TPU:24, one launch (start us, length us, event | category | flops | bytes accessed | tf_op | source)
XLA Modules:
  0.0 108.1 jit_solution(15297497901871680269)
XLA Ops:
  0.0 106.1 %shard_map.17 = bf16[2048,1024]{1,0:T(8,128)(2,1)S(1)} custom-call(s32[2048,1024]{1,0:T(8,128)} %adj_hbm.1), custom_call_target="tpu_custom_call" | custom-call | tf_op jit(solution)/shard_map/pallas_call | solution.py:247
  106.1 2.0 %copy.3 = bf16[2048,1024]{1,0:T(8,128)(2,1)} copy(bf16[2048,1024]{1,0:T(8,128)(2,1)S(1)} %shard_map.17) | data formatting | bytes 8388608

commit v3 on v2

--- a/solution.py
+++ b/solution.py
@@ -13,16 +13,17 @@
 CHUNK = 32
 RIGHT = 64
 GROUP = 256
+TAIL = 128
 TILE = 256
 PER_STEP = 2
 MESH = pl.DeviceIdType.MESH
 
 
 def lag_of(row):
-    return (5 * row) // 2
-
-
-def kernel(n_rows, n_cols, window, adj_hbm, out, adj, left, right,
+    return 1 + (5 * row) // 2
+
+
+def kernel(n_rows, n_cols, window, adj_hbm, out, adj, left, right, partial,
            adj_sem, z_send, z_recv, x_send, x_recv, r_send, r_recv):
     block_rows, block_cols = adj.shape
     holders = left.shape[0]
@@ -77,45 +78,49 @@
             src_ref=part, dst_ref=part, send_sem=r_send, recv_sem=r_recv.at[i],
             device_id={"row": r + 1}, device_id_type=MESH)
 
-    @pl.loop(0, n_adj)
+    adj_copy(0).start()
+
+    barrier = pltpu.get_barrier_semaphore()
+
+    def greet(where):
+        pl.semaphore_signal(barrier, inc=1, device_id=where, device_id_type=MESH)
+
+    @pl.when(hi > 0)
+    def _():
+        greet({"col": c - holders})
+
+    @pl.when(hi < stages - 1)
+    def _():
+        greet({"col": c + holders})
+
+    for d in range(1, holders):
+        greet({"col": hi * holders + lax.rem(lo + d, holders)})
+
+    @pl.when(r > 0)
+    def _():
+        greet({"row": r - 1})
+
+    @pl.when(r < n_rows - 1)
+    def _():
+        greet({"row": r + 1})
+
+    def convert_left(j):
+        left[lo, chunk(j), :] = adj[chunk(j), :].astype(jnp.bfloat16)
+
+    def convert_right(i):
+        right[r_rows(i), :] = adj[r_rows(i), :].astype(jnp.bfloat16)
+
+    ahead = RIGHT // CHUNK
+    adj_copy(0).wait()
+
+    @pl.loop(1, n_adj)
     def _(i):
         adj_copy(i).start()
 
-    barrier = pltpu.get_barrier_semaphore()
-
-    def greet(where):
-        pl.semaphore_signal(barrier, inc=1, device_id=where, device_id_type=MESH)
-
-    @pl.when(hi > 0)
-    def _():
-        greet({"col": c - holders})
-
-    @pl.when(hi < stages - 1)
-    def _():
-        greet({"col": c + holders})
-
-    for d in range(1, holders):
-        greet({"col": hi * holders + lax.rem(lo + d, holders)})
-
-    @pl.when(r > 0)
-    def _():
-        greet({"row": r - 1})
-
-    @pl.when(r < n_rows - 1)
-    def _():
-        greet({"row": r + 1})
-
-    def convert_left(j):
-        left[lo, chunk(j), :] = adj[chunk(j), :].astype(jnp.bfloat16)
-
-    def convert_right(i):
-        right[r_rows(i), :] = adj[r_rows(i), :].astype(jnp.bfloat16)
-
-    adj_copy(0).wait()
-
     @pl.when(hi == 0)
     def _():
-        convert_left(0)
+        for k in range(ahead):
+            convert_left(k)
 
     @pl.when(r == 0)
     def _():
@@ -126,18 +131,6 @@
     pl.semaphore_wait(barrier, known)
 
     def step(j):
-        @pl.when(j + 1 < n_adj)
-        def _():
-            adj_copy(j + 1).wait()
-
-        @pl.when((hi == 0) & (j + 1 < n_chunks))
-        def _():
-            convert_left(j + 1)
-
-        @pl.when((r == 0) & (j + 1 < n_right))
-        def _():
-            convert_right(j + 1)
-
         @pl.when(hi > 0)
         def _():
             z_copy(j).wait_recv()
@@ -160,6 +153,18 @@
             @pl.when(r < n_rows - 1)
             def _():
                 r_copy(i).start()
+
+        @pl.when(j + 1 < n_adj)
+        def _():
+            adj_copy(j + 1).wait()
+
+        @pl.when((hi == 0) & (j + ahead < n_chunks))
+        def _():
+            convert_left(j + ahead)
+
+        @pl.when((r == 0) & (j + 1 < n_right))
+        def _():
+            convert_right(j + 1)
 
     def compute(u):
         g = u // n_tiles
@@ -214,9 +219,35 @@
             def _():
                 r_copy(i).start()
 
-    @pl.loop(done, units)
+    @pl.loop(done, body_units)
     def _(u):
         compute(u)
+
+    def arrived(start):
+        for d in range(1, holders):
+            @pl.loop(start // CHUNK, (start + TAIL) // CHUNK)
+            def _(k):
+                x_arrival(d, k).wait_recv()
+
+    def half(h, start, cols):
+        rights = pl.ds(pl.multiple_of(h * block_cols, block_cols), block_cols)
+        return jnp.dot(left[h, start:start + TAIL, :], right[rights, cols], preferred_element_type=jnp.float32)
+
+    tiles = [slice(t * TILE, (t + 1) * TILE) for t in range(n_tiles)]
+    for start in range(block_rows - GROUP, block_rows, TAIL):
+        last = start + TAIL == block_rows
+        if not last:
+            arrived(start)
+        for cols in tiles:
+            partial[:, cols] = half(lo, start, cols)
+        if last:
+            arrived(start)
+        for cols in tiles:
+            counts = partial[:, cols]
+            for d in range(1, holders):
+                counts += half(lax.rem(lo + holders - d, holders), start, cols)
+            out[start:start + TAIL, cols] = jnp.where(
+                counts > 0.5, 1, adj[start:start + TAIL, cols]).astype(out.dtype)
 
     whole = left.at[lo]
 
@@ -253,6 +284,7 @@
             pltpu.VMEM((block_rows, block_cols), jnp.int32),
             pltpu.VMEM((holders, block_rows, block_cols), jnp.bfloat16),
             pltpu.VMEM((window, block_cols), jnp.bfloat16),
+            pltpu.VMEM((TAIL, block_cols), jnp.float32),
             dma((block_rows // RIGHT,)),
             dma,
             dma((n_chunks,)),

time: 108 us -> 107 us (level)
  Pallas kernels: 106 us -> 104 us
    pallas_call x1, Pallas kernels: 106 us -> 104 us  [per_device(): pl.pallas_call(functools.partial(kernel, n_rows, n_cols, window), out_sha...]
where the time goes in v3:
time: 107 us; the launch traced here: 106 us
  Pallas kernels  104 us (97%)
  local copies, waits for them, and re-layouts  2.02 us (2%)
    pallas_call x1, Pallas kernels, per_device(): pl.pallas_call(functools.partial(kernel, n_rows, n_cols, window), out_sha...  104 us

profile of v3, /device:TPU:24, one launch (start us, length us, event | category | flops | bytes accessed | tf_op | source)
XLA Modules:
  0.0 106.5 jit_solution(16475106491540226755)
XLA Ops:
  0.0 104.5 %shard_map.17 = bf16[2048,1024]{1,0:T(8,128)(2,1)S(1)} custom-call(s32[2048,1024]{1,0:T(8,128)} %adj_hbm.1), custom_call_target="tpu_custom_call" | custom-call | tf_op jit(solution)/shard_map/pallas_call | solution.py:278
  104.5 2.0 %copy.3 = bf16[2048,1024]{1,0:T(8,128)(2,1)} copy(bf16[2048,1024]{1,0:T(8,128)(2,1)S(1)} %shard_map.17) | data formatting | bytes 8388608

commit v4 on v3

--- a/solution.py
+++ b/solution.py
@@ -24,7 +24,7 @@
 
 
 def kernel(n_rows, n_cols, window, adj_hbm, out, adj, left, right, partial,
-           adj_sem, z_send, z_recv, x_send, x_recv, r_send, r_recv):
+           adj_sem, z_send, b_send, z_recv, x_send, x_recv, r_send, r_recv):
     block_rows, block_cols = adj.shape
     holders = left.shape[0]
     stages = n_cols // holders
@@ -42,6 +42,12 @@
     lo = lax.rem(c, holders)
     lag = lag_of(r)
 
+    relay = lax.rem(hi, 2) == 0
+    feeds_next = relay & (hi < stages - 1)
+    feeds_back = relay & (hi > 0)
+    next_col = c + holders * (1 + (hi + 2 < stages).astype(jnp.int32))
+    back_col = c - holders
+
     def adj_copy(i):
         rows = pl.ds(pl.multiple_of(i * RIGHT, RIGHT), RIGHT)
         return pltpu.make_async_copy(adj_hbm.at[rows], adj.at[rows], adj_sem.at[i])
@@ -53,7 +59,13 @@
         part = left.at[lo, chunk(j)]
         return pltpu.make_async_remote_copy(
             src_ref=part, dst_ref=part, send_sem=z_send, recv_sem=z_recv.at[j],
-            device_id={"col": c + holders}, device_id_type=MESH)
+            device_id={"col": next_col}, device_id_type=MESH)
+
+    def z_back(j):
+        part = left.at[lo, chunk(j)]
+        return pltpu.make_async_remote_copy(
+            src_ref=part, dst_ref=part, send_sem=b_send, recv_sem=z_recv.at[j],
+            device_id={"col": back_col}, device_id_type=MESH)
 
     def x_copy(d, j):
         part = left.at[lo, chunk(j)]
@@ -85,13 +97,22 @@
     def greet(where):
         pl.semaphore_signal(barrier, inc=1, device_id=where, device_id_type=MESH)
 
-    @pl.when(hi > 0)
+    @pl.when(feeds_back)
+    def _():
+        greet({"col": c - 2 * holders})
+        greet({"col": back_col})
+
+    @pl.when(feeds_next)
+    def _():
+        greet({"col": next_col})
+
+    @pl.when(~relay & (hi < stages - 1))
+    def _():
+        greet({"col": c + holders})
+
+    @pl.when(~relay & (hi == stages - 1))
     def _():
         greet({"col": c - holders})
-
-    @pl.when(hi < stages - 1)
-    def _():
-        greet({"col": c + holders})
 
     for d in range(1, holders):
         greet({"col": hi * holders + lax.rem(lo + d, holders)})
@@ -126,7 +147,8 @@
     def _():
         convert_right(0)
 
-    known = ((hi > 0).astype(jnp.int32) + (hi < stages - 1).astype(jnp.int32) + (holders - 1)
+    known = (2 * feeds_back.astype(jnp.int32) + feeds_next.astype(jnp.int32)
+             + (~relay).astype(jnp.int32) + (holders - 1)
              + (r > 0).astype(jnp.int32) + (r < n_rows - 1).astype(jnp.int32))
     pl.semaphore_wait(barrier, known)
 
@@ -135,9 +157,13 @@
         def _():
             z_copy(j).wait_recv()
 
-        @pl.when(hi < stages - 1)
+        @pl.when(feeds_next)
         def _():
             z_copy(j).start()
+
+        @pl.when(feeds_back)
+        def _():
+            z_back(j).start()
 
         for d in range(1, holders):
             x_copy(d, j).start()
@@ -251,11 +277,17 @@
 
     whole = left.at[lo]
 
-    @pl.when(hi < stages - 1)
+    @pl.when(feeds_next)
     def _():
         pltpu.make_async_remote_copy(
             src_ref=whole, dst_ref=whole, send_sem=z_send, recv_sem=z_recv.at[0],
-            device_id={"col": c + holders}, device_id_type=MESH).wait_send()
+            device_id={"col": next_col}, device_id_type=MESH).wait_send()
+
+    @pl.when(feeds_back)
+    def _():
+        pltpu.make_async_remote_copy(
+            src_ref=whole, dst_ref=whole, send_sem=b_send, recv_sem=z_recv.at[0],
+            device_id={"col": back_col}, device_id_type=MESH).wait_send()
 
     for d in range(1, holders):
         pltpu.make_async_remote_copy(
@@ -287,6 +319,7 @@
             pltpu.VMEM((TAIL, block_cols), jnp.float32),
             dma((block_rows // RIGHT,)),
             dma,
+            dma,
             dma((n_chunks,)),
             dma((holders - 1,)),
             dma((holders - 1, n_chunks)),

time: 107 us -> 106 us (level)
    pallas_call x1, Pallas kernels: 104 us -> 103 us  [per_device(): pl.pallas_call(functools.partial(kernel, n_rows, n_cols, window), out_sha...]
where the time goes in v4:
time: 106 us; the launch traced here: 105 us
  Pallas kernels  103 us (97%)
  local copies, waits for them, and re-layouts  2.02 us (2%)
    pallas_call x1, Pallas kernels, per_device(): pl.pallas_call(functools.partial(kernel, n_rows, n_cols, window), out_sha...  103 us

profile of v4, /device:TPU:24, one launch (start us, length us, event | category | flops | bytes accessed | tf_op | source)
XLA Modules:
  0.0 104.5 jit_solution(12167492871304637196)
XLA Ops:
  0.0 102.5 %shard_map.17 = bf16[2048,1024]{1,0:T(8,128)(2,1)S(1)} custom-call(s32[2048,1024]{1,0:T(8,128)} %adj_hbm.1), custom_call_target="tpu_custom_call" | custom-call | tf_op jit(solution)/shard_map/pallas_call | solution.py:310
  102.5 2.0 %copy.3 = bf16[2048,1024]{1,0:T(8,128)(2,1)} copy(bf16[2048,1024]{1,0:T(8,128)(2,1)S(1)} %shard_map.17) | data formatting | bytes 8388608

commit v5 on v4

--- a/solution.py
+++ b/solution.py
@@ -14,8 +14,8 @@
 RIGHT = 64
 GROUP = 256
 TAIL = 128
-TILE = 256
-PER_STEP = 2
+TILE = 512
+PER_STEP = 1
 MESH = pl.DeviceIdType.MESH
 
 

time: 106 us -> 106 us (level)
  no operation moved by 1% of the time
where the time goes in v5:
time: 106 us; the launch traced here: 104 us
  Pallas kernels  102 us (96%)
  local copies, waits for them, and re-layouts  2.02 us (2%)
    pallas_call x1, Pallas kernels, per_device(): pl.pallas_call(functools.partial(kernel, n_rows, n_cols, window), out_sha...  102 us

profile of v5, /device:TPU:24, one launch (start us, length us, event | category | flops | bytes accessed | tf_op | source)
XLA Modules:
  0.0 104.4 jit_solution(15914776235213862271)
XLA Ops:
  0.0 102.3 %shard_map.17 = bf16[2048,1024]{1,0:T(8,128)(2,1)S(1)} custom-call(s32[2048,1024]{1,0:T(8,128)} %adj_hbm.1), custom_call_target="tpu_custom_call" | custom-call | tf_op jit(solution)/shard_map/pallas_call | solution.py:310
  102.3 2.0 %copy.3 = bf16[2048,1024]{1,0:T(8,128)(2,1)} copy(bf16[2048,1024]{1,0:T(8,128)(2,1)S(1)} %shard_map.17) | data formatting | bytes 8388608
